TPU v7x, 128 devices: a whole 4x4x4 slice. The times are simulated.
128 devices in a mesh: row: 8 (over x_hi, z), col: 16 (over x_lo, y, core).
Axes of the slice: x: 4 (x_hi: 2, x_lo: 2; x = x_hi * 2 + x_lo), y: 4, z: 4, core: 2. Of those that a mesh axis runs over, the one named last changes fastest.
Arguments:
- features: bfloat16 [384, 256, 512], P('row', 'col'), may hold values from -12 to 12
- cotangent: bfloat16 [384, 256, 512], P('row', 'col'), may hold values from -6 to 6
- w_query: bfloat16 [512, 512], replicated, may hold values from -0.53033009 to 0.53033009
- w_key: bfloat16 [512, 512], replicated, may hold values from -0.53033009 to 0.53033009
- w_value: bfloat16 [512, 512], replicated, may hold values from -0.25 to 0.25
- w_out: bfloat16 [512, 512], replicated, may hold values from -0.25 to 0.25
Outputs:
- layer_out: bfloat16 [384, 256, 512], P('row', 'col')
- grad_features: bfloat16 [384, 256, 512], P('row', 'col')
- grad_query: float32 [512, 512], replicated
- grad_key: float32 [512, 512], replicated
- grad_value: float32 [512, 512], replicated
- grad_proj: float32 [512, 512], replicated
All inputs are finite; a program needn't handle non-finite values.
Results may differ from a plain program's by a relative error of at most 0.012.
The roundings to bfloat16 on the way count: a program that leaves them out, or rounds other values in their place, can miss the bound.
Values may be sent and summed in bfloat16 or wider, within the bound.
A program may use at most 128 MiB of HBM per device.

v0:
```python
import jax
import jax.numpy as jnp
from jax import lax
from jax.sharding import PartitionSpec as P

HEADS = 8
NEG_FILL = -1e30


def passed_along(block, axis, distance):
    devices = range(lax.axis_size(axis))
    route = [((i - distance) % len(devices), i) for i in devices]
    return lax.ppermute(block, axis, route)


def sent_together(arrays, axis, dim, along):
    both = jnp.concatenate(arrays, axis=along)
    filled, at, finished = (lax.all_gather(both, axis, axis=dim, tiled=True), 0, [])
    for a in arrays:
        finished.append(lax.slice_in_dim(filled, at, at + a.shape[along], axis=along))
        at += a.shape[along]
    return tuple(finished)


def product_of(form, left, right):
    return jnp.einsum(form, left, right, preferred_element_type=jnp.float32)


def project(left, weight):
    return jnp.dot(left, weight, preferred_element_type=jnp.float32).astype(jnp.bfloat16)


def times_transposed(left, weight):
    return lax.dot_general(
        left, weight, (((1,), (1,)), ((), ())), preferred_element_type=jnp.float32
    )


def inner_sum(left, right):
    return lax.dot_general(
        left, right, (((0,), (0,)), ((), ())), preferred_element_type=jnp.float32
    )


def inner_exact(left, right):
    return lax.dot_general(
        left,
        right,
        (((0,), (0,)), ((), ())),
        precision=lax.Precision.HIGHEST,
        preferred_element_type=jnp.float32,
    )


def transposed_exact(left, weight):
    return lax.dot_general(
        left,
        weight.astype(jnp.float32),
        (((1,), (1,)), ((), ())),
        precision=lax.Precision.HIGHEST,
        preferred_element_type=jnp.float32,
    )


def to_windows(field):
    tile_rows, tile_cols, feature = field.shape
    blocks = field.reshape(tile_rows // 16, 16, tile_cols // 16, 16, feature)
    return blocks.transpose(0, 2, 1, 3, 4).reshape(-1, 256, feature)


def from_windows(blocks, tile_rows, tile_cols):
    feature = blocks.shape[-1]
    field = blocks.reshape(tile_rows // 16, tile_cols // 16, 16, 16, feature)
    return field.transpose(0, 2, 1, 3, 4).reshape(tile_rows, tile_cols, feature)


def split_heads(field, heads):
    blocks = to_windows(field)
    count, per_window, feature = blocks.shape
    return blocks.reshape(count, per_window, heads, feature // heads).transpose(2, 0, 1, 3)


def join_heads(stacked, tile_rows, tile_cols):
    heads, count, per_window, depth = stacked.shape
    blocks = stacked.transpose(1, 2, 0, 3).reshape(count, per_window, heads * depth)
    return from_windows(blocks, tile_rows, tile_cols)


def summary_heads(table, heads):
    count, feature = table.shape
    return table.reshape(count, heads, feature // heads).transpose(1, 0, 2)


def join_summary(stacked):
    heads, count, depth = stacked.shape
    return stacked.transpose(1, 0, 2).reshape(count, heads * depth)


def region_allowed(row_flag, col_flag):
    region = row_flag.astype(jnp.int32)[:, None] * 2 + col_flag.astype(jnp.int32)[None, :]
    blocks = to_windows(region[:, :, None])[:, :, 0]
    return blocks[:, :, None] == blocks[:, None, :]


def pool_field(field):
    tile_rows, tile_cols, feature = field.shape
    blocks = field.astype(jnp.float32).reshape(tile_rows // 8, 8, tile_cols // 8, 8, feature)
    return jnp.mean(blocks, axis=(1, 3)).reshape(-1, feature).astype(jnp.bfloat16)


def spread_pool(grad_pooled, tile_rows, tile_cols):
    feature = grad_pooled.shape[-1]
    blocks = grad_pooled.reshape(tile_rows // 8, 1, tile_cols // 8, 1, feature) / 64.0
    blocks = jnp.broadcast_to(blocks, (tile_rows // 8, 8, tile_cols // 8, 8, feature))
    return blocks.reshape(tile_rows, tile_cols, feature)


def one_head(operands, allowed, scale):
    queries, keys_win, values_win, summary_keys, summary_values, grad_attn = operands
    scores_win = jnp.where(allowed, product_of("wid,wjd->wij", queries, keys_win) * scale, NEG_FILL)
    scores_sum = product_of("wid,md->wim", queries, summary_keys) * scale
    highest = jnp.maximum(jnp.max(scores_win, axis=-1), jnp.max(scores_sum, axis=-1))[..., None]
    expo_win = jnp.exp(scores_win - highest)
    expo_sum = jnp.exp(scores_sum - highest)
    denominator = jnp.sum(expo_win, axis=-1, keepdims=True) + jnp.sum(
        expo_sum, axis=-1, keepdims=True
    )
    probs_win = expo_win / denominator
    probs_sum = expo_sum / denominator
    weights_win = probs_win.astype(jnp.bfloat16)
    weights_sum = probs_sum.astype(jnp.bfloat16)
    attended = product_of("wij,wjd->wid", weights_win, values_win) + product_of(
        "wim,md->wid", weights_sum, summary_values
    )
    dprob_win = product_of("wid,wjd->wij", grad_attn, values_win)
    dprob_sum = product_of("wid,md->wim", grad_attn, summary_values)
    inner = jnp.sum(probs_win * dprob_win, axis=-1, keepdims=True) + jnp.sum(
        probs_sum * dprob_sum, axis=-1, keepdims=True
    )
    dscore_win = (probs_win * (dprob_win - inner) * scale).astype(jnp.bfloat16)
    dscore_sum = (probs_sum * (dprob_sum - inner) * scale).astype(jnp.bfloat16)
    grad_q = product_of("wij,wjd->wid", dscore_win, keys_win) + product_of(
        "wim,md->wid", dscore_sum, summary_keys
    )
    grad_k = product_of("wij,wid->wjd", dscore_win, queries)
    grad_v = product_of("wij,wid->wjd", weights_win, grad_attn)
    grad_sk = product_of("wim,wid->md", dscore_sum, queries)
    grad_sv = product_of("wim,wid->md", weights_sum, grad_attn)
    return (
        attended.astype(jnp.bfloat16),
        grad_q.astype(jnp.bfloat16),
        grad_k.astype(jnp.bfloat16),
        grad_v.astype(jnp.bfloat16),
        grad_sk,
        grad_sv,
    )


def attend(queries, keys, values, summary_keys, summary_values, grad_attn, allowed, heads):
    tile_rows, tile_cols, feature = queries.shape
    scale = float(feature // heads) ** (-0.5)
    operands = (
        split_heads(queries, heads),
        split_heads(keys, heads),
        split_heads(values, heads),
        summary_heads(summary_keys, heads),
        summary_heads(summary_values, heads),
        split_heads(grad_attn, heads),
    )
    results = lax.map(lambda stacked: one_head(stacked, allowed, scale), operands)
    attended, grad_q, grad_k, grad_v, grad_sk, grad_sv = results
    return (
        join_heads(attended, tile_rows, tile_cols),
        join_heads(grad_q, tile_rows, tile_cols),
        join_heads(grad_k, tile_rows, tile_cols),
        join_heads(grad_v, tile_rows, tile_cols),
        join_summary(grad_sk),
        join_summary(grad_sv),
    )


def body(features, cotangent, w_query, w_key, w_value, w_out):
    tile_rows, tile_cols, feature = features.shape
    upper = passed_along(features[tile_rows - 8 :], "row", 1)
    stacked = jnp.concatenate([upper, features[: tile_rows - 8]], axis=0)
    leftmost = passed_along(stacked[:, tile_cols - 8 :], "col", 1)
    shifted = jnp.concatenate([leftmost, stacked[:, : tile_cols - 8]], axis=1)
    flat = shifted.reshape(-1, feature)
    queries = project(flat, w_query).reshape(shifted.shape)
    keys = project(flat, w_key).reshape(shifted.shape)
    values = project(flat, w_value).reshape(shifted.shape)
    pooled = pool_field(shifted)
    local_keys = project(pooled, w_key)
    local_values = project(pooled, w_value)
    summary_keys, summary_values = sent_together((local_keys, local_values), ("row", "col"), 0, 1)
    grad_flat = cotangent.reshape(-1, feature)
    grad_attn = times_transposed(grad_flat, w_out).astype(jnp.bfloat16).reshape(shifted.shape)
    row_flag = (jnp.arange(tile_rows) < 8) & (lax.axis_index("row") == 0)
    col_flag = (jnp.arange(tile_cols) < 8) & (lax.axis_index("col") == 0)
    allowed = region_allowed(row_flag, col_flag)
    attended, grad_q, grad_k, grad_v, part_sk, part_sv = attend(
        queries, keys, values, summary_keys, summary_values, grad_attn, allowed, HEADS
    )
    attended_flat = attended.reshape(-1, feature)
    layer_out = (
        (
            flat.astype(jnp.float32)
            + jnp.dot(attended_flat, w_out, preferred_element_type=jnp.float32)
        )
        .astype(jnp.bfloat16)
        .reshape(shifted.shape)
    )
    grad_q = grad_q.reshape(-1, feature)
    grad_k = grad_k.reshape(-1, feature)
    grad_v = grad_v.reshape(-1, feature)
    grad_query = inner_sum(flat, grad_q)
    grad_key = inner_sum(flat, grad_k)
    grad_value = inner_sum(flat, grad_v)
    grad_proj = inner_sum(attended_flat, grad_flat)
    grad_sk, grad_sv = (
        lax.psum_scatter(part_sk, ("row", "col"), scatter_dimension=0, tiled=True),
        lax.psum_scatter(part_sv, ("row", "col"), scatter_dimension=0, tiled=True),
    )
    grad_pooled = transposed_exact(grad_sk, w_key) + transposed_exact(grad_sv, w_value)
    pooled_wide = pooled.astype(jnp.float32)
    grad_key = grad_key + inner_exact(pooled_wide, grad_sk)
    grad_value = grad_value + inner_exact(pooled_wide, grad_sv)
    grad_query, grad_key, grad_value, grad_proj = lax.psum(
        (grad_query, grad_key, grad_value, grad_proj), ("row", "col")
    )
    local_part = (
        times_transposed(grad_q, w_query)
        + times_transposed(grad_k, w_key)
        + times_transposed(grad_v, w_value)
    )
    grad_field = (
        cotangent.astype(jnp.float32)
        + local_part.reshape(shifted.shape)
        + spread_pool(grad_pooled, tile_rows, tile_cols)
    )
    return (layer_out, grad_field.astype(jnp.bfloat16), grad_query, grad_key, grad_value, grad_proj)


def solution(mesh):
    placed = (P("row", "col", None), P("row", "col", None), P(), P(), P(), P())
    return jax.shard_map(
        body,
        mesh=mesh,
        in_specs=placed,
        out_specs=(P("row", "col", None), P("row", "col", None), P(), P(), P(), P()),
        check_vma=False,
    )
```

profile of v0, /device:TPU:1, one launch (start us, length us, event | category | flops | bytes accessed | tf_op | source)
XLA Modules:
  0.0 729.4 jit_solution(13153387075901120608)
XLA Ops:
  8.3 2.5 collective-permute-start
  11.9 6.6 collective-permute-done
  18.6 2.5 collective-permute-start.1
  21.1 4.7 collective-permute-done.1
  27.6 1.6 convolution_convert_fusion.2
  30.8 2.3 copy.71
  33.1 1.6 convolution_convert_fusion.5
  41.5 2.3 copy.69
  48.1 174.9 %all-gather.3.cloned.1.call-done = bf16[128,12,1024]{2,1,0:T(8,128)(2,1)} async-done(((bf16[1,12,1024]{2,1,0:T(8,128)(2,1)}), bf16[128,12,1024]{2,1,0:T(8,128)(2,1)}) %all-gather.3.cloned.1.call-update) | async-done | bytes 3145744 | tf_op jit(solution)/shard_map/all_gather | solution.py:18
  223.0 6.1 reshape.139
  229.1 3.7 fusion.103
  232.8 1.7 copy.64
  234.6 2.6 copy.66
  237.2 161.6 %while.21 = (s32[]{:T(128)}, bf16[8,3,256,64]{2,3,1,0:T(8,128)(2,1)}, bf16[8,3,256,64]{2,3,1,0:T(8,128)(2,1)}, bf16[8,3,256,64]{2,3,1,0:T(8,128)(2,1)}, bf16[8,3...) while((s32[]{:T(128)}, ...), condition=%wide.region_8.9_spmd.clone, body=%wide.region_1.8_spmd.clone.sunk | while | flops 1091073792 | bytes 59510444 | solution.py:170
  240.4 1.9 fusion.197
  243.6 2.4 multiply_reduce_fusion.7
  246.0 1.5 multiply_convert_fusion.5
  250.8 1.7 fusion.193
  254.6 2.8 fusion.191
  260.6 1.9 fusion.197
  263.8 2.4 multiply_reduce_fusion.7
  266.2 1.5 multiply_convert_fusion.5
  271.0 1.7 fusion.193
  274.8 2.8 fusion.191
  280.8 2.0 fusion.197
  284.0 2.4 multiply_reduce_fusion.7
  286.4 1.5 multiply_convert_fusion.5
  291.2 1.7 fusion.193
  295.0 2.8 fusion.191
  301.1 2.0 fusion.197
  304.2 2.4 multiply_reduce_fusion.7
  311.4 1.7 fusion.193
  315.2 2.8 fusion.191
  321.3 1.9 fusion.197
  324.5 2.4 multiply_reduce_fusion.7
  326.9 1.5 multiply_convert_fusion.5
  331.6 1.7 fusion.193
  335.5 2.8 fusion.191
  341.5 1.9 fusion.197
  344.7 2.4 multiply_reduce_fusion.7
  351.8 1.7 fusion.193
  355.6 2.8 fusion.191
  361.7 1.9 fusion.197
  364.8 2.4 multiply_reduce_fusion.7
  372.0 1.7 fusion.193
  375.8 2.8 fusion.191
  381.9 1.9 fusion.197
  385.0 2.4 multiply_reduce_fusion.7
  392.2 1.7 fusion.193
  396.0 2.8 fusion.191
  402.7 2.1 copy.72
  405.0 1.6 fusion.106
  406.6 1.5 fusion.107
  408.2 147.8 %all-reduce.9.cloned.1.call-done = (f32[1536,512]{0,1:T(8,128)}, f32[1536,512]{0,1:T(8,128)}) async-done(((f32[1536,512]{0,1:T(8,128)}, f32[1536,512]{0,1:T(8,128)}), (f32[1536,512]{0,1:T(8,128)}, f32[1536,512]{0,1:T(8,128)})) %all-reduce.9.cloned.1.call-update) | async-done | bytes 6291472
  556.0 1.7 fusion.89
  557.7 1.7 fusion.92
  559.5 1.6 convolution_add_fusion.1
  561.1 1.6 convolution_add_fusion.2
  562.7 1.9 fusion.104
  567.3 1.8 fusion.94
  569.2 1.9 fusion.86
  572.6 143.6 %all-reduce.7.cloned.1.call-done = (f32[512,512]{1,0:T(8,128)}, f32[512,512]{1,0:T(8,128)}, f32[512,512]{1,0:T(8,128)}, f32[512,512]{1,0:T(8,128)}) async-done(((f32[512,512]{1,0:T(8,128)}, f32[512,512]{1,0:T(8,128)}, f32[512,512]{1,0:T(8,128)}, f32[512,512]{1,0:T(8,128)}), (f32[512,512]{1,0:T(8,128)}, f32[512,512]{1,0:T(8,128)}, f32[512,512]{1,0:T(8,128)}, ...) | async-done | bytes 4194320 | tf_op jit(solution)/shard_map/psum | solution.py:228
  716.2 2.4 copy.123
  718.6 2.3 copy.124
  (228 shorter events, 110.9 us)
Async XLA Ops:
  7.2 19.2 %copy-start = (bf16[512,512]{1,0:T(8,128)(2,1)S(1)}, bf16[512,512]{1,0:T(8,128)(2,1)}, u32[]{:S(2)}) copy-start(bf16[512,512]{1,0:T(8,128)(2,1)} %param.11) | copy-start | bytes 1572868
  7.2 19.0 %copy-start.4 = (bf16[512,512]{1,0:T(8,128)(2,1)S(1)}, bf16[512,512]{1,0:T(8,128)(2,1)}, u32[]{:S(2)}) copy-start(bf16[512,512]{1,0:T(8,128)(2,1)} %param.12) | copy-start | bytes 1572868
  7.2 215.8 %all-gather.3.cloned.1.call-start = ((), (), s32[]{:S(2)}) async-start(), calls=%async_computation | async-start | bytes 4227072 | tf_op jit(solution)/shard_map/all_gather | solution.py:18
  8.2 19.3 %copy-start.6 = (bf16[48,16,512]{2,1,0:T(8,128)(2,1)S(1)}, bf16[48,16,512]{2,1,0:T(8,128)(2,1)}, u32[]{:S(2)}) copy-start(bf16[48,16,512]{2,1,0:T(8,128)(2,1)} %param.9) | copy-start | bytes 2359300
  8.3 10.3 %collective-permute-start = (bf16[8,16,512]{2,1,0:T(8,128)(2,1)S(1)}, bf16[8,16,512]{2,1,0:T(8,128)(2,1)S(1)}, u32[]{:S(2)}, u32[]{:S(2)}) collective-permute-start(bf16[8,16,512]{2,1,0:T(8,128)(2,1)S(1)} %slice.18), channel_id=1, source_target_pairs={{112,0},{0,16},{16,32},{32,48},{48,64},{64,80},{80,96},{96,112},{1... | collective-permute-start | bytes 393224 | tf_op jit(solution)/shard_map/ppermute | solution.py:13
  18.6 7.2 collective-permute-start.1
  25.9 17.9 %copy-start.1 = (bf16[48,16,512]{2,1,0:T(8,128)(2,1)}, bf16[48,16,512]{2,1,0:T(8,128)(2,1)S(1)}, u32[]{:S(2)}) copy-start(bf16[48,16,512]{2,1,0:T(8,128)(2,1)S(1)} %fusion.87) | copy-start | bytes 2359300
  26.2 1.4 copy-start.18
  27.2 528.8 %all-reduce.9.cloned.1.call-start = ((), (), s32[]{:S(2)}) async-start(), calls=%async_computation.2 | async-start | bytes 12582912
  239.3 1.1 copy-start.13
  259.5 1.1 copy-start.13
  279.7 1.1 copy-start.13
  299.9 1.1 copy-start.13
  320.2 1.1 copy-start.13
  340.4 1.1 copy-start.13
  360.5 1.1 copy-start.13
  380.7 1.1 copy-start.13
  398.8 1.1 copy-start.16
  398.8 2.0 copy-start.15
  398.9 317.4 %all-reduce.7.cloned.1.call-start = ((), (), s32[]{:S(2)}) async-start(), calls=%async_computation.1 | async-start | bytes 8388608 | tf_op jit(solution)/shard_map/psum | solution.py:228
  400.6 1.1 copy-start.14
  402.5 2.6 copy-start.2
  402.6 4.0 copy-start.3
  402.7 4.0 copy-start.7
  404.8 151.1 %copy-start.19 = (bf16[12,512]{1,0:T(8,128)(2,1)S(1)}, bf16[12,512]{1,0:T(8,128)(2,1)}, u32[]{:S(2)}) copy-start(bf16[12,512]{1,0:T(8,128)(2,1)} %copy-done.18) | copy-start | bytes 36868
  405.0 1.6 copy-start.9
  561.1 1.6 copy-start.17
  562.7 2.5 copy-start.10
  562.7 2.5 copy-start.20
  564.6 2.1 copy-start.5
  567.3 3.9 copy-start.8
  716.2 4.7 copy-start.12
  716.2 5.7 copy-start.11
Sparse Core Ops, SparseCore 0:
  27.3 195.6 all-gather.2
  399.0 156.9 all-reduce.8
  562.8 153.3 all-reduce.6
where the time goes:
time: 732 us; the launch traced here: 729 us
  waiting for transfers between devices  478 us (65%)
  matrix products  163 us (22%)
  local copies, waits for them, and re-layouts  44.1 us (6%)
  other arithmetic  24.6 us (3%)
  between operations  14.2 us (2%)
    all_gather x1, waiting for transfers between devices, sent_together(): lax.all_gather(both, axis, axis=dim, tiled=True)  175 us
    unnamed x4, waiting for transfers between devices  148 us
    psum x1, waiting for transfers between devices, body(): lax.psum((grad_query, grad_key, grad_value, grad_proj), ('row', 'col'))  144 us
    dot_general x96, matrix products, product_of(): return jnp.einsum(form, left, right, preferred_element_type=jnp.float32)  138 us
    unnamed x53, local copies, waits for them, and re-layouts  21.4 us
  transfers between devices with their start and end apart: 5, of which 5 were waited for; matrix products, arithmetic and copies ran while one was open for 5% of the time, Pallas kernels for 0%

commit v1 on v0

--- a/solution.py
+++ b/solution.py
@@ -226,7 +226,7 @@
     grad_key = grad_key + inner_exact(pooled_wide, grad_sk)
     grad_value = grad_value + inner_exact(pooled_wide, grad_sv)
     grad_query, grad_key, grad_value, grad_proj = lax.psum(
-        (grad_query, grad_key, grad_value, grad_proj), ("row", "col")
+        lax.psum((grad_query, grad_key, grad_value, grad_proj), "col"), "row"
     )
     local_part = (
         times_transposed(grad_q, w_query)

time: 732 us -> 843 us (1.15)
  waiting for transfers between devices: 478 us -> 549 us
  matrix products: 163 us -> 186 us
  local copies, waits for them, and re-layouts: 44.1 us -> 57.7 us
    psum x1 -> x2, waiting for transfers between devices: 144 us -> 229 us  [the longest x1 127 us: body(): lax.psum((grad_query, grad_key, grad_value, grad_proj), 'col')]
    dot_general x96, matrix products: 138 us -> 160 us  [product_of(): return jnp.einsum(form, left, right, preferred_element_type=jnp.float32)]
    all_gather x1, waiting for transfers between devices: 175 us -> 162 us  [sent_together(): lax.all_gather(both, axis, axis=dim, tiled=True)]
    unnamed x4 -> x5, waiting for transfers between devices: 148 us -> 147 us
  transfers between devices with their start and end apart: 5 -> 6, of which waited for: 5 -> 6; matrix products, arithmetic and copies ran while one was open for 5% -> 7% of each run, Pallas kernels for 0% -> 0%
where the time goes in v1:
time: 843 us; the launch traced here: 839 us
  waiting for transfers between devices  549 us (65%)
  matrix products  186 us (22%)
  local copies, waits for them, and re-layouts  57.7 us (7%)
  other arithmetic  26 us (3%)
  between operations  14.2 us (2%)
    all_gather x1, waiting for transfers between devices, sent_together(): lax.all_gather(both, axis, axis=dim, tiled=True)  162 us
    dot_general x96, matrix products, product_of(): return jnp.einsum(form, left, right, preferred_element_type=jnp.float32)  160 us
    unnamed x5, waiting for transfers between devices  147 us
    psum x1, waiting for transfers between devices, body(): lax.psum((grad_query, grad_key, grad_value, grad_proj), 'col')  127 us
    psum x1, waiting for transfers between devices, body(): lax.psum(lax.psum((grad_query, grad_key, grad_value, grad_proj), 'col'),...  102 us
    unnamed x53, local copies, waits for them, and re-layouts  22.3 us
  transfers between devices with their start and end apart: 6, of which 6 were waited for; matrix products, arithmetic and copies ran while one was open for 7% of the time, Pallas kernels for 0%

profile of v1, /device:TPU:1, one launch (start us, length us, event | category | flops | bytes accessed | tf_op | source)
XLA Modules:
  0.0 839.3 jit_solution(15378676171327434913)
XLA Ops:
  8.3 2.5 collective-permute-start
  11.9 6.6 collective-permute-done
  18.6 2.5 collective-permute-start.1
  21.1 4.7 collective-permute-done.1
  27.6 2.6 convolution_convert_fusion.2
  30.2 2.4 copy.67
  32.6 3.4 reshape_reshape_transpose_reshape_reshape.27
  35.9 2.3 copy.71
  39.7 2.3 copy.62
  42.0 3.4 reshape_reshape_transpose_reshape_reshape.24
  45.4 2.3 copy.68
  49.1 2.3 copy.63
  51.4 3.4 reshape_reshape_transpose_reshape_reshape.25
  54.8 2.3 copy.69
  61.4 161.8 %all-gather.3.cloned.1.call-done = bf16[128,12,1024]{2,1,0:T(8,128)(2,1)} async-done(((bf16[1,12,1024]{2,1,0:T(8,128)(2,1)}), bf16[128,12,1024]{2,1,0:T(8,128)(2,1)}) %all-gather.3.cloned.1.call-update) | async-done | bytes 3145744 | tf_op jit(solution)/shard_map/all_gather | solution.py:18
  223.1 6.1 reshape.139
  229.3 3.7 fusion.103
  234.7 2.6 copy.66
  237.3 183.4 %while.21 = (s32[]{:T(128)}, bf16[8,3,256,64]{2,3,1,0:T(8,128)(2,1)}, bf16[8,3,256,64]{2,3,1,0:T(8,128)(2,1)}, bf16[8,3,256,64]{2,3,1,0:T(8,128)(2,1)}, bf16[8,3...) while((s32[]{:T(128)}, ...), condition=%wide.region_8.9_spmd.clone, body=%wide.region_1.8_spmd.clone.sunk | while | flops 1091073792 | bytes 59510444 | solution.py:170
  241.5 1.9 fusion.197
  244.7 2.4 multiply_reduce_fusion.7
  248.6 2.2 fusion.196
  251.0 1.8 fusion.194
  257.5 2.8 fusion.191
  264.4 1.9 fusion.197
  267.6 2.4 multiply_reduce_fusion.7
  271.5 2.2 fusion.196
  273.9 1.8 fusion.194
  280.4 2.8 fusion.191
  287.4 1.9 fusion.197
  290.5 2.4 multiply_reduce_fusion.7
  294.4 2.2 fusion.196
  303.3 2.8 fusion.191
  310.3 1.9 fusion.197
  313.4 2.4 multiply_reduce_fusion.7
  317.3 2.2 fusion.196
  319.7 1.8 fusion.194
  326.2 2.8 fusion.191
  333.2 1.9 fusion.197
  336.3 2.4 multiply_reduce_fusion.7
  340.3 2.2 fusion.196
  349.1 2.8 fusion.191
  356.1 2.0 fusion.197
  359.3 2.4 multiply_reduce_fusion.7
  363.2 2.2 fusion.196
  372.0 2.8 fusion.191
  379.0 1.9 fusion.197
  382.2 2.4 multiply_reduce_fusion.7
  386.1 2.2 fusion.196
  395.0 2.8 fusion.191
  401.9 1.9 fusion.197
  405.1 2.4 multiply_reduce_fusion.7
  409.0 2.2 fusion.196
  417.9 2.8 fusion.191
  422.7 1.9 copy.74
  425.6 2.1 copy.72
  431.1 146.6 %all-reduce.9.cloned.1.call-done = (f32[1536,512]{0,1:T(8,128)}, f32[1536,512]{0,1:T(8,128)}) async-done(((f32[1536,512]{0,1:T(8,128)}, f32[1536,512]{0,1:T(8,128)}), (f32[1536,512]{0,1:T(8,128)}, f32[1536,512]{0,1:T(8,128)})) %all-reduce.9.cloned.1.call-update) | async-done | bytes 6291472
  584.5 127.4 %all-reduce.11.cloned.1.call-done = (f32[512,512]{1,0:T(8,128)}, f32[512,512]{1,0:T(8,128)}, f32[512,512]{1,0:T(8,128)}, f32[512,512]{1,0:T(8,128)}) async-done(((f32[512,512]{1,0:T(8,128)}, f32[512,512]{1,0:T(8,128)}, f32[512,512]{1,0:T(8,128)}, f32[512,512]{1,0:T(8,128)}), (f32[512,512]{1,0:T(8,128)}, f32[512,512]{1,0:T(8,128)}, f32[512,512]{1,0:T(8,128)}, ...) | async-done | bytes 4194320 | tf_op jit(solution)/shard_map/psum | solution.py:229
  712.0 1.9 fusion.104
  717.8 1.8 fusion.94
  721.7 2.8 add_convert_fusion
  724.4 101.8 %all-reduce.13.cloned.1.call-done = (f32[512,512]{1,0:T(8,128)}, f32[512,512]{1,0:T(8,128)}, f32[512,512]{1,0:T(8,128)}, f32[512,512]{1,0:T(8,128)}) async-done(((f32[512,512]{1,0:T(8,128)}, f32[512,512]{1,0:T(8,128)}, f32[512,512]{1,0:T(8,128)}, f32[512,512]{1,0:T(8,128)}), (f32[512,512]{1,0:T(8,128)}, f32[512,512]{1,0:T(8,128)}, f32[512,512]{1,0:T(8,128)}, ...) | async-done | bytes 4194320 | tf_op jit(solution)/shard_map/psum | solution.py:228
  826.2 2.4 copy.127
  828.6 2.3 copy.128
  (231 shorter events, 136.8 us)
Async XLA Ops:
  7.2 19.2 %copy-start = (bf16[512,512]{1,0:T(8,128)(2,1)S(1)}, bf16[512,512]{1,0:T(8,128)(2,1)}, u32[]{:S(2)}) copy-start(bf16[512,512]{1,0:T(8,128)(2,1)} %param.11) | copy-start | bytes 1572868
  7.2 19.0 %copy-start.4 = (bf16[512,512]{1,0:T(8,128)(2,1)S(1)}, bf16[512,512]{1,0:T(8,128)(2,1)}, u32[]{:S(2)}) copy-start(bf16[512,512]{1,0:T(8,128)(2,1)} %param.12) | copy-start | bytes 1572868
  7.2 215.9 %all-gather.3.cloned.1.call-start = ((), (), s32[]{:S(2)}) async-start(), calls=%async_computation | async-start | bytes 4227072 | tf_op jit(solution)/shard_map/all_gather | solution.py:18
  8.2 19.3 %copy-start.19 = (bf16[512,512]{1,0:T(8,128)(2,1)S(1)}, bf16[512,512]{1,0:T(8,128)(2,1)}, u32[]{:S(2)}) copy-start(bf16[512,512]{1,0:T(8,128)(2,1)} %param.13) | copy-start | bytes 1572868
  8.3 10.3 %collective-permute-start = (bf16[8,16,512]{2,1,0:T(8,128)(2,1)S(1)}, bf16[8,16,512]{2,1,0:T(8,128)(2,1)S(1)}, u32[]{:S(2)}, u32[]{:S(2)}) collective-permute-start(bf16[8,16,512]{2,1,0:T(8,128)(2,1)S(1)} %slice.18), channel_id=1, source_target_pairs={{112,0},{0,16},{16,32},{32,48},{48,64},{64,80},{80,96},{96,112},{1... | collective-permute-start | bytes 393224 | tf_op jit(solution)/shard_map/ppermute | solution.py:13
  18.6 7.2 collective-permute-start.1
  25.9 31.2 %copy-start.1 = (bf16[48,16,512]{2,1,0:T(8,128)(2,1)}, bf16[48,16,512]{2,1,0:T(8,128)(2,1)S(1)}, u32[]{:S(2)}) copy-start(bf16[48,16,512]{2,1,0:T(8,128)(2,1)S(1)} %fusion.87) | copy-start | bytes 2359300
  26.2 9.8 %copy-start.17 = (bf16[12,512]{1,0:T(8,128)(2,1)}, bf16[12,512]{1,0:T(8,128)(2,1)S(1)}, u32[]{:S(2)}) copy-start(bf16[12,512]{1,0:T(8,128)(2,1)S(1)} %convert_element_type.86) | copy-start | bytes 36868
  27.2 550.6 %all-reduce.9.cloned.1.call-start = ((), (), s32[]{:S(2)}) async-start(), calls=%async_computation.1 | async-start | bytes 12582912
  30.2 8.1 copy-start.15
  240.4 1.1 copy-start.12
  263.3 1.1 copy-start.12
  286.2 1.1 copy-start.12
  309.1 1.1 copy-start.12
  332.0 1.1 copy-start.12
  355.0 1.1 copy-start.12
  377.9 1.1 copy-start.12
  400.8 1.1 copy-start.12
  420.7 1.1 copy-start.14
  420.7 291.3 %all-reduce.11.cloned.1.call-start = ((), (), s32[]{:S(2)}) async-start(), calls=%async_computation.2 | async-start | bytes 8388608 | tf_op jit(solution)/shard_map/psum | solution.py:229
  422.5 2.2 copy-start.13
  425.4 2.6 copy-start.2
  425.6 4.0 copy-start.3
  425.6 4.0 copy-start.6
  427.8 150.0 %copy-start.18 = (bf16[12,512]{1,0:T(8,128)(2,1)S(1)}, bf16[12,512]{1,0:T(8,128)(2,1)}, u32[]{:S(2)}) copy-start(bf16[12,512]{1,0:T(8,128)(2,1)} %copy-done.17) | copy-start | bytes 36868
  428.0 1.6 copy-start.8
  584.5 127.5 %copy-start.16 = (bf16[512,512]{1,0:T(8,128)(2,1)S(1)}, bf16[512,512]{1,0:T(8,128)(2,1)}, u32[]{:S(2)}) copy-start(bf16[512,512]{1,0:T(8,128)(2,1)} %param.10) | copy-start | bytes 1572868
  584.5 241.7 %all-reduce.13.cloned.1.call-start = ((), (), s32[]{:S(2)}) async-start(), calls=%async_computation.3 | async-start | bytes 8388608 | tf_op jit(solution)/shard_map/psum | solution.py:228
  712.0 2.5 copy-start.9
  712.0 2.5 copy-start.20
  713.9 2.1 copy-start.5
  717.8 3.8 copy-start.7
  826.2 4.7 copy-start.11
  826.2 5.7 copy-start.10
Sparse Core Ops, SparseCore 0:
  27.3 195.8 all-gather.2
  420.8 156.8 all-reduce.8
  584.6 127.3 all-reduce.10
  714.6 111.5 all-reduce.12
